TPU v7x, 32 devices: a whole 2x2x4 slice. The times are simulated.
32 devices in a mesh: batch: 4 (over y, x), heads: 8 (over z, core).
Axes of the slice: x: 2, y: 2, z: 4, core: 2. Of those that a mesh axis runs over, the one named last changes fastest.
Arguments:
- draft_ids: int32 [192, 8], P('batch'), may hold values from 0 to 50279
- accepted: int32 [192], P('batch'), may hold values from 1 to 8
- embedding: bfloat16 [50280, 2560], P(None, 'heads'), may hold values from -6 to 6
- norm_gain: float32 [2, 2560], replicated, may hold values from 0.5 to 1.5
- w_zx: bfloat16 [2, 2560, 8, 128], P(None, None, 'heads'), may hold values from -0.125 to 0.125
- w_dt: bfloat16 [2, 2560, 8], P(None, None, 'heads'), may hold values from -0.125 to 0.125
- w_bc: bfloat16 [2, 2560, 256], P(None, None, 'heads'), may hold values from -0.125 to 0.125
- dt_bias: float32 [2, 8], P(None, 'heads'), may hold values from -4 to -1
- decay_rate: float32 [2, 8], P(None, 'heads'), may hold values from 1 to 16
- skip_weight: float32 [2, 8], P(None, 'heads'), may hold values from 0.5 to 1.5
- conv_x_w: bfloat16 [2, 4, 512], P(None, None, 'heads'), may hold values from -3 to 3
- conv_x_b: bfloat16 [2, 512], P(None, 'heads'), may hold values from -3 to 3
- conv_bc_w: bfloat16 [2, 4, 256], P(None, None, 'heads'), may hold values from -3 to 3
- conv_bc_b: bfloat16 [2, 256], P(None, 'heads'), may hold values from -3 to 3
- gate_gain: float32 [2, 512], P(None, 'heads'), may hold values from 0.5 to 1.5
- out_w: bfloat16 [2, 512, 2560], P(None, 'heads'), may hold values from -0.375 to 0.375
- ssm_state: float32 [2, 192, 8, 64, 128], P(None, 'batch', 'heads'), may hold values from -1.6 to 1.6
- conv_x_state: bfloat16 [2, 192, 3, 512], P(None, 'batch', None, 'heads'), may hold values from -6 to 6
- conv_bc_state: bfloat16 [2, 192, 3, 256], P(None, 'batch', None, 'heads'), may hold values from -6 to 6
Outputs:
- hidden_out: bfloat16 [1536, 2560], P('batch', 'heads')
- new_ssm: float32 [2, 192, 8, 64, 128], P(None, 'batch', 'heads')
- new_conv_x: bfloat16 [2, 192, 3, 512], P(None, 'batch', None, 'heads')
- new_conv_bc: bfloat16 [2, 192, 3, 256], P(None, 'batch', None, 'heads')
Inputs may be any that keep to these rules, and one draw needn't show every extreme that they name: `accepted`: the number of a sequence's draft tokens that are kept, counted from the first.
All inputs are finite; a program needn't handle non-finite values.
Results may differ from a plain program's by a relative error of at most 0.015.
Values may be sent and summed in bfloat16 or wider, within the bound.
A program may use at most 128 MiB of HBM per device.

v0:
```python
import jax
import jax.numpy as jnp
from jax import lax
from jax.sharding import PartitionSpec as P

LAYERS = 2
EPS = 1e-05


def rms_scale(total, count):
    return lax.rsqrt(total / count + EPS)


def convolve(window, weight, bias, count):
    weight = weight.astype(jnp.float32)
    acc = window[:, 0:count] * weight[0]
    for k in range(1, weight.shape[0]):
        acc = acc + window[:, k : k + count] * weight[k]
    return jax.nn.silu(acc + bias.astype(jnp.float32))


def keep_rows(window, accepted, kept_rows):
    last_start = window.shape[1] - kept_rows
    kept = window[:, 1 : 1 + kept_rows]
    for start in range(2, last_start + 1):
        kept = jnp.where(
            (accepted == start)[:, None, None], window[:, start : start + kept_rows], kept
        )
    return kept


def recur(decay, step, values, bmat, cmat, skip, state, accepted):
    kept = state
    outputs = []
    for t in range(values.shape[1]):
        state = (
            decay[:, t, None, None] * state
            + (step[:, t, None] * values[:, t])[:, :, None] * bmat[:, t, None, :]
        )
        outputs.append(jnp.sum(state * cmat[:, t, None, :], axis=-1) + skip * values[:, t])
        kept = jnp.where((accepted == t + 1)[:, None, None], state, kept)
    return (jnp.stack(outputs, 1), kept)


def spread_terms(u_rows, scale, weight):
    product = lax.dot_general(
        weight, u_rows, (((0,), (1,)), ((), ())), preferred_element_type=jnp.float32
    )
    return product * scale[None, :]


def token_scale(local_sq, inner):
    return rms_scale(lax.psum(local_sq, "heads"), inner)


def local(
    draft_ids,
    accepted,
    embedding,
    norm_gain,
    w_zx,
    w_dt,
    w_bc,
    dt_bias,
    decay_rate,
    skip_weight,
    conv_x_w,
    conv_x_b,
    conv_bc_w,
    conv_bc_b,
    gate_gain,
    out_w,
    ssm_state,
    conv_x_state,
    conv_bc_state,
):
    seq_rows, draft = draft_ids.shape
    heads_here = w_zx.shape[2]
    width = w_zx.shape[3] // 2
    local_inner = heads_here * width
    own_cols = embedding.shape[1]
    model = own_cols * lax.axis_size("heads")
    inner = local_inner * lax.axis_size("heads")
    bc_here = w_bc.shape[2]
    kernel = conv_x_w.shape[1]
    recur_heads = jax.vmap(recur, in_axes=(2, 2, 2, None, None, 0, 1, None), out_axes=(2, 1))
    whole_bc = (
        lax.all_gather(w_bc, "heads", axis=2, tiled=True),
        lax.all_gather(conv_bc_w, "heads", axis=2, tiled=True),
        lax.all_gather(conv_bc_b, "heads", axis=1, tiled=True),
        lax.all_gather(conv_bc_state, "heads", axis=3, tiled=True),
    )
    saved_state, saved_x, saved_bc = ([], [], [])

    def mixer(layer, stream):
        value = stream.astype(jnp.float32)
        normed = (
            value * rms_scale(jnp.sum(value * value, -1, keepdims=True), model) * norm_gain[layer]
        ).astype(jnp.bfloat16)
        zx = jnp.dot(
            normed, w_zx[layer].reshape(model, -1), preferred_element_type=jnp.float32
        ).astype(jnp.bfloat16)
        zx = zx.reshape(seq_rows, draft, heads_here, 2, width)
        gate_z = zx[:, :, :, 0].astype(jnp.float32)
        values = zx[:, :, :, 1].reshape(seq_rows, draft, local_inner)
        dt_raw = (
            jnp.dot(normed, w_dt[layer], preferred_element_type=jnp.float32)
            .astype(jnp.bfloat16)
            .reshape(seq_rows, draft, heads_here)
        )
        bc = (
            jnp.dot(normed, whole_bc[0][layer], preferred_element_type=jnp.float32)
            .astype(jnp.bfloat16)
            .reshape(seq_rows, draft, -1)
        )
        window_bc = jnp.concatenate([whole_bc[3][layer], bc], axis=1)
        bcc = convolve(
            window_bc.astype(jnp.float32), whole_bc[1][layer], whole_bc[2][layer], draft
        ).astype(jnp.bfloat16)
        kept_bc = keep_rows(window_bc, accepted, kernel - 1)
        bcc = lax.optimization_barrier(bcc).astype(jnp.float32)
        kept_bc = lax.dynamic_slice_in_dim(kept_bc, lax.axis_index("heads") * bc_here, bc_here, 2)
        states = bcc.shape[2] // 2
        bmat = bcc[..., :states]
        cmat = bcc[..., states:]
        window_x = jnp.concatenate([conv_x_state[layer], values], axis=1)
        xc = convolve(
            window_x.astype(jnp.float32), conv_x_w[layer], conv_x_b[layer], draft
        ).reshape(seq_rows, draft, heads_here, width)
        step = jax.nn.softplus(dt_raw.astype(jnp.float32) + dt_bias[layer])
        decay = jnp.exp(-step * decay_rate[layer])
        outputs, kept = recur_heads(
            decay, step, xc, bmat, cmat, skip_weight[layer], ssm_state[layer], accepted
        )
        saved_state.append(kept)
        saved_x.append(keep_rows(window_x, accepted, kernel - 1))
        saved_bc.append(kept_bc)
        gated = outputs * jax.nn.silu(gate_z)
        local_sq = jnp.sum(gated * gated, axis=(2, 3)).reshape(-1)
        u_rows = (
            (gated.reshape(seq_rows, draft, local_inner) * gate_gain[layer])
            .astype(jnp.bfloat16)
            .reshape(-1, local_inner)
        )
        return (u_rows, local_sq)

    part = embedding[draft_ids.reshape(-1)]
    stream = lax.all_gather(part, "heads", axis=1, tiled=True)
    where_cols = lax.axis_index("heads") * own_cols
    result = part
    for layer in range(LAYERS):
        u_rows, local_sq = mixer(layer, stream)
        scale = token_scale(local_sq, inner)
        if layer + 1 < LAYERS:
            term = (
                jnp.dot(u_rows, out_w[layer], preferred_element_type=jnp.float32) * scale[:, None]
            )
            total = lax.psum(term, "heads")
            stream = (stream.astype(jnp.float32) + total).astype(jnp.bfloat16)
        else:
            mine = lax.psum_scatter(
                spread_terms(u_rows, scale, out_w[layer]), "heads", scatter_dimension=0, tiled=True
            )
            own_stream = lax.dynamic_slice_in_dim(stream, where_cols, own_cols, 1)
            result = (own_stream.astype(jnp.float32) + mine.T).astype(jnp.bfloat16)
    return (result, jnp.stack(saved_state), jnp.stack(saved_x), jnp.stack(saved_bc))


def solution(mesh):
    placed = (
        P("batch", None),
        P("batch"),
        P(None, "heads"),
        P(),
        P(None, None, "heads", None),
        P(None, None, "heads"),
        P(None, None, "heads"),
        P(None, "heads"),
        P(None, "heads"),
        P(None, "heads"),
        P(None, None, "heads"),
        P(None, "heads"),
        P(None, None, "heads"),
        P(None, "heads"),
        P(None, "heads"),
        P(None, "heads", None),
        P(None, "batch", "heads", None, None),
        P(None, "batch", None, "heads"),
        P(None, "batch", None, "heads"),
    )
    return jax.shard_map(
        local,
        mesh=mesh,
        in_specs=placed,
        out_specs=(
            P("batch", "heads"),
            P(None, "batch", "heads", None, None),
            P(None, "batch", None, "heads"),
            P(None, "batch", None, "heads"),
        ),
        check_vma=False,
    )
```

profile of v0, /device:TPU:0, one launch (start us, length us, event | category | flops | bytes accessed | tf_op | source)
XLA Modules:
  0.0 371.8 jit_solution(4346947506731001234)
XLA Ops:
  7.2 43.7 %copy.113 = bf16[50280,320]{1,0:T(8,128)(2,1)} copy(bf16[50280,320]{0,1:T(8,128)(2,1)} %param.21) | data formatting | bytes 64358400 | tf_op args[2]
  51.2 7.8 %gather_fusion = bf16[384,320]{1,0:T(8,128)(2,1)S(1)} fusion(bf16[50280,320]{1,0:T(8,128)(2,1)} %copy.113, s32[1024]{0:T(1024)S(1)} %pad_clamp_fusion), kind=kCustom, calls=%fused_computation | custom fusion | bytes 493056 | tf_op jit(solution)/shard_map/gather | solution.py:147
  60.8 16.7 %all_gather.16 = bf16[2,48,3,256]{1,3,2,0:T(8,128)(2,1)S(1)} all-gather(bf16[2,48,3,32]{1,3,2,0:T(8,128)(2,1)S(1)} %copy-done.48), channel_id=1, replica_groups=mesh['batch'=4,'heads'=8] {'heads'}, dimensions={3}, use_global_device_ids=true | all-gather | bytes 165888 | tf_op jit(solution)/shard_map/all_gather | solution.py:91
  77.9 15.1 %all_gather.18 = bf16[2,4,256]{1,0,2:T(2,128)(2,1)S(1)} all-gather(bf16[2,4,32]{1,0,2:T(2,128)(2,1)S(1)} %copy.118), channel_id=1, replica_groups=mesh['batch'=4,'heads'=8] {'heads'}, dimensions={2}, use_global_device_ids=true | all-gather | bytes 4608 | tf_op jit(solution)/shard_map/all_gather | solution.py:89
  93.0 12.0 %all-gather.1 = bf16[8,32,2]{1,2,0:T(2,128)(2,1)S(1)} all-gather(bf16[1,32,2]{1,2,0:T(2,128)(2,1)S(1)} %bitcast.580), channel_id=1, replica_groups=mesh['batch'=4,'heads'=8] {'heads'}, dimensions={0}, use_global_device_ids=true | all-gather | bytes 1152 | tf_op jit(solution)/shard_map/all_gather | solution.py:90
  107.1 2.9 slice_reduce_fusion.7
  111.3 2.7 copy.115
  119.7 7.5 %all-gather.5.cloned.1.call-done = bf16[2,2560,256]{1,2,0:T(8,128)(2,1)} async-done(((bf16[2,2560,32]{1,2,0:T(8,128)(2,1)}), bf16[2,2560,256]{1,2,0:T(8,128)(2,1)}) %all-gather.5.cloned.1.call-update) | async-done | bytes 2621456 | tf_op jit(solution)/shard_map/all_gather | solution.py:88
  127.2 2.0 fusion.15
  130.1 1.1 copy-done
  131.2 4.1 %multiply_add_fusion.8 = (f32[1,48,64,128]{3,2,1,0:T(8,128)S(1)}, f32[1,48,64,128]{3,2,1,0:T(8,128)S(1)}, f32[48,64]{1,0:T(8,128)S(1)}, f32[48,64]{1,0:T(8,128)S(1)}) fusion(f32[48,128]{1,0:T(8,128)S(1)} %bitcast.537, f32[48,64]{1,0:T(8,128)S(1)} %get-tuple-element.186, f32[48]{0:T(128)S(1)} %get-tuple-element.237, f32[48,128]{1,0:T(8,128)S(1)} %bitcast.525, ...), kind=kLoop, calls=%fused_computation.43 | loop fusion | flops 7464960 | bytes 4977600 | tf_op jit(solution)/shard_map/vmap()/add | solution.py:37
  136.0 1.6 multiply_reduce_fusion.12
  139.5 3.7 multiply_reduce_fusion.8
  145.9 15.0 %psum.21 = f32[384]{0:T(512)S(1)} all-reduce(f32[384]{0:T(512)S(1)} %reshape.2511), channel_id=1, replica_groups=mesh['batch'=4,'heads'=8] {'heads'}, use_global_device_ids=true, to_apply=%region_10.11 | all-reduce | flops 384 | bytes 3072 | tf_op jit(solution)/shard_map/psum | solution.py:53
  160.9 3.5 convolution_multiply_fusion.1
  165.6 2.9 slice_reduce_fusion.3
  168.5 85.9 %all-reduce.2.cloned.1.call-done = f32[384,2560]{1,0:T(8,128)} async-done(((f32[384,2560]{1,0:T(8,128)}), f32[384,2560]{1,0:T(8,128)}) %all-reduce.2.cloned.1.call-update) | async-done | bytes 3932176 | tf_op jit(solution)/shard_map/psum | solution.py:158
  254.3 2.9 fusion.1
  259.4 1.0 fusion.121
  264.7 2.1 fusion.14
  267.6 1.0 bitcast_multiply_fusion.2
  268.8 4.1 %multiply_add_fusion.2 = (f32[1,48,64,128]{3,2,1,0:T(8,128)S(1)}, f32[1,48,64,128]{3,2,1,0:T(8,128)S(1)}, f32[48,64]{1,0:T(8,128)S(1)}, f32[48,64]{1,0:T(8,128)S(1)}) fusion(f32[48,128]{1,0:T(8,128)S(1)} %bitcast.551, f32[48,64]{1,0:T(8,128)S(1)} %get-tuple-element.160, f32[48]{0:T(128)S(1)} %get-tuple-element.51, f32[48,128]{1,0:T(8,128)S(1)} %bitcast.528, ...), kind=kLoop, calls=%fused_computation.29 | loop fusion | flops 7464960 | bytes 4977600 | tf_op jit(solution)/shard_map/vmap()/add | solution.py:37
  273.0 1.2 constant_dynamic-update-slice_fusion.23
  274.2 1.6 multiply_reduce_fusion.4
  275.9 1.2 constant_dynamic-update-slice_fusion.22
  277.1 1.2 constant_dynamic-update-slice_fusion.21
  278.3 1.2 constant_dynamic-update-slice_fusion.20
  279.5 3.7 multiply_reduce_fusion
  283.2 1.2 constant_dynamic-update-slice_fusion.19
  284.4 1.2 constant_dynamic-update-slice_fusion.18
  285.6 1.2 constant_dynamic-update-slice_fusion.17
  286.7 1.9 constant_dynamic-update-slice_fusion.16
  290.3 15.7 %psum.23 = f32[384]{0:T(512)S(1)} all-reduce(f32[384]{0:T(512)S(1)} %reshape.2516), channel_id=1, replica_groups=mesh['batch'=4,'heads'=8] {'heads'}, use_global_device_ids=true, to_apply=%region_22.23 | all-reduce | flops 384 | bytes 3072 | tf_op jit(solution)/shard_map/psum | solution.py:53
  306.0 1.1 fusion.71
  307.1 3.5 fusion
  310.6 5.6 %copy.139 = f32[2560,384]{1,0:T(8,128)} copy(f32[2560,384]{0,1:T(8,128)} %fusion) | data formatting | bytes 7864320
  316.2 1.2 broadcast_compare_fusion.7
  317.5 1.7 fusion.105
  319.1 1.4 fusion.119
  322.0 9.0 %select_select_fusion.1 = f32[1,48,1,64,128]{4,3,2,1,0:T(8,128)} fusion(f32[2,48,1,64,128]{4,3,2,1,0:T(8,128)S(1)} %copy-done.1, f32[48,128]{1,0:T(8,128)} %bitcast.536, f32[48,64]{1,0:T(8,128)} %copy-done.34, f32[48,128]{1,0:T(8,128)} %bitcast.534, f32[48,64]{1,0:T(8,128)} %copy-done.35, f32[48,128]{1,0:T(8,128)} %bitcast.532, f32[48,64]{1,0:T(8,128)} %copy-done.33, ...), kind=kLoop, calls=%fused_computation.22 | loop fusion | flops 12582912 | bytes 3442560 | tf_op jit(solution)/shard_map/vmap(jit(_where))/select_n | solution.py:41
  332.4 1.4 pad_maximum_fusion.6
  333.8 0.9 fusion.106
  334.7 1.4 pad_maximum_fusion.5
  336.1 8.2 %select_select_fusion = f32[1,48,1,64,128]{4,3,2,1,0:T(8,128)S(1)} fusion(f32[2,48,1,64,128]{4,3,2,1,0:T(8,128)S(1)} %copy-done.1, f32[48,128]{1,0:T(8,128)} %bitcast.550, f32[48,64]{1,0:T(8,128)} %copy-done.40, f32[48,128]{1,0:T(8,128)} %bitcast.548, f32[48,64]{1,0:T(8,128)} %copy-done.42, f32[48,128]{1,0:T(8,128)} %bitcast.546, f32[48,64]{1,0:T(8,128)} %copy-done.41, ...), kind=kLoop, calls=%fused_computation.21 | loop fusion | flops 12582912 | bytes 3442560 | tf_op jit(solution)/shard_map/vmap(jit(_where))/select_n | solution.py:41
  344.4 1.9 pad_maximum_fusion
  346.3 15.7 %reduce-scatter.4.cloned.1.call-done = f32[320,384]{1,0:T(8,128)} async-done(((f32[2560,384]{1,0:T(8,128)}), f32[320,384]{1,0:T(8,128)}) %reduce-scatter.4.cloned.1.call-update) | async-done | bytes 491536
  361.9 1.3 copy.140
  363.2 1.2 fusion.20
  (259 shorter events, 30.2 us)
Async XLA Ops:
  7.2 43.8 %copy-start.73 = (s32[48,8]{0,1:T(8,128)S(1)}, s32[48,8]{0,1:T(8,128)}, u32[]{:S(2)}) copy-start(s32[48,8]{0,1:T(8,128)} %param.19) | copy-start | bytes 4612
  7.2 104.1 %all-gather.7.cloned.1.call-start = ((), (), s32[]{:S(2)}) async-start(), calls=%async_computation.3 | async-start | bytes 2211840 | tf_op jit(solution)/shard_map/all_gather | solution.py:148
  51.2 9.7 %copy-start.48 = (bf16[2,48,3,32]{1,3,2,0:T(8,128)(2,1)S(1)}, bf16[2,48,3,32]{1,3,2,0:T(8,128)(2,1)}, u32[]{:S(2)}) copy-start(bf16[2,48,3,32]{1,3,2,0:T(8,128)(2,1)} %param.37) | copy-start | bytes 55300
  59.0 18.7 %copy-start.75 = (bf16[2,4,32]{2,1,0:T(4,128)(2,1)S(1)}, bf16[2,4,32]{2,1,0:T(4,128)(2,1)}, u32[]{:S(2)}) copy-start(bf16[2,4,32]{2,1,0:T(4,128)(2,1)} %param.31) | copy-start | bytes 1540
  59.0 34.0 %copy-start.82 = (bf16[2,32]{1,0:T(2,128)(2,1)S(1)}, bf16[2,32]{1,0:T(2,128)(2,1)}, u32[]{:S(2)}) copy-start(bf16[2,32]{1,0:T(2,128)(2,1)} %param.32) | copy-start | bytes 388
  59.0 46.1 %copy-start.77 = (f32[2,1]{0,1:T(1,128)S(1)}, f32[2,1]{0,1:T(1,128)}, u32[]{:S(2)}) copy-start(f32[2,1]{0,1:T(1,128)} %param.26) | copy-start | bytes 28
  59.0 46.7 %copy-start.78 = (f32[2,1]{0,1:T(1,128)S(1)}, f32[2,1]{0,1:T(1,128)}, u32[]{:S(2)}) copy-start(f32[2,1]{0,1:T(1,128)} %param.27) | copy-start | bytes 28
  59.1 47.3 %copy-start.79 = (f32[2,1]{0,1:T(1,128)S(1)}, f32[2,1]{0,1:T(1,128)}, u32[]{:S(2)}) copy-start(f32[2,1]{0,1:T(1,128)} %param.28) | copy-start | bytes 28
  59.1 47.8 %copy-start.55 = (f32[2,2560]{1,0:T(2,128)S(1)}, f32[2,2560]{1,0:T(2,128)}, u32[]{:S(2)}) copy-start(f32[2,2560]{1,0:T(2,128)} %param.22) | copy-start | bytes 61444
  60.0 50.1 %copy-start.80 = (bf16[2,64]{1,0:T(2,128)(2,1)S(1)}, bf16[2,64]{1,0:T(2,128)(2,1)}, u32[]{:S(2)}) copy-start(bf16[2,64]{1,0:T(2,128)(2,1)} %param.30) | copy-start | bytes 772
  60.0 50.1 %copy-start.81 = (f32[2,64]{1,0:T(2,128)S(1)}, f32[2,64]{1,0:T(2,128)}, u32[]{:S(2)}) copy-start(f32[2,64]{1,0:T(2,128)} %param.33) | copy-start | bytes 1540
  60.0 51.2 %copy-start.76 = (bf16[2,4,64]{2,1,0:T(4,128)(2,1)S(1)}, bf16[2,4,64]{2,1,0:T(4,128)(2,1)}, u32[]{:S(2)}) copy-start(bf16[2,4,64]{2,1,0:T(4,128)(2,1)} %param.29) | copy-start | bytes 3076
  60.0 51.2 %copy-start.47 = (bf16[2,48,3,64]{3,1,2,0:T(8,128)(2,1)S(1)}, bf16[2,48,3,64]{3,1,2,0:T(8,128)(2,1)}, u32[]{:S(2)}) copy-start(bf16[2,48,3,64]{3,1,2,0:T(8,128)(2,1)} %param.36) | copy-start | bytes 110596
  60.0 67.2 %all-gather.5.cloned.1.call-start = ((), (), s32[]{:S(2)}) async-start(), calls=%async_computation.1 | async-start | bytes 2949120 | tf_op jit(solution)/shard_map/all_gather | solution.py:88
  60.8 193.6 %all-reduce.2.cloned.1.call-start = ((), (), s32[]{:S(2)}) async-start(), calls=%async_computation.2 | async-start | bytes 7864320 | tf_op jit(solution)/shard_map/psum | solution.py:158
  77.8 51.5 %copy-start.10 = (bf16[48,3,256]{2,1,0:T(4,128)(2,1)}, bf16[48,3,256]{2,1,0:T(4,128)(2,1)S(1)}, u32[]{:S(2)}) copy-start(bf16[48,3,256]{2,1,0:T(4,128)(2,1)S(1)} %copy.117) | copy-start | bytes 221188
  111.3 149.2 %copy-start.17 = (bf16[48,3,64]{2,0,1:T(8,128)(2,1)}, bf16[48,3,64]{2,0,1:T(8,128)(2,1)S(1)}, u32[]{:S(2)}) copy-start(bf16[48,3,64]{2,0,1:T(8,128)(2,1)S(1)} %get-tuple-element.193) | copy-start | bytes 55300
  119.2 10.8 %copy-start.58 = (f32[48]{0:T(128)}, f32[48]{0:T(128)S(1)}, u32[]{:S(2)}) copy-start(f32[48]{0:T(128)S(1)} %get-tuple-element.233) | copy-start | bytes 580
  119.2 10.8 %copy-start.59 = (f32[48]{0:T(128)}, f32[48]{0:T(128)S(1)}, u32[]{:S(2)}) copy-start(f32[48]{0:T(128)S(1)} %get-tuple-element.234) | copy-start | bytes 580
  119.2 10.8 %copy-start.60 = (f32[48]{0:T(128)}, f32[48]{0:T(128)S(1)}, u32[]{:S(2)}) copy-start(f32[48]{0:T(128)S(1)} %get-tuple-element.235) | copy-start | bytes 580
  119.3 10.8 %copy-start.61 = (f32[48]{0:T(128)}, f32[48]{0:T(128)S(1)}, u32[]{:S(2)}) copy-start(f32[48]{0:T(128)S(1)} %get-tuple-element.237) | copy-start | bytes 580
  119.3 16.7 %copy-start.56 = (f32[48]{0:T(128)}, f32[48]{0:T(128)S(1)}, u32[]{:S(2)}) copy-start(f32[48]{0:T(128)S(1)} %get-tuple-element.236) | copy-start | bytes 580
  119.3 20.1 %copy-start.66 = (f32[48]{0:T(128)}, f32[48]{0:T(128)S(1)}, u32[]{:S(2)}) copy-start(f32[48]{0:T(128)S(1)} %get-tuple-element.238) | copy-start | bytes 580
  119.3 20.1 %copy-start.67 = (f32[48]{0:T(128)}, f32[48]{0:T(128)S(1)}, u32[]{:S(2)}) copy-start(f32[48]{0:T(128)S(1)} %get-tuple-element.239) | copy-start | bytes 580
  119.3 20.1 %copy-start.68 = (f32[48]{0:T(128)}, f32[48]{0:T(128)S(1)}, u32[]{:S(2)}) copy-start(f32[48]{0:T(128)S(1)} %get-tuple-element.240) | copy-start | bytes 580
  119.6 10.5 %copy-start.36 = (f32[48,64]{1,0:T(8,128)}, f32[48,64]{1,0:T(8,128)S(1)}, u32[]{:S(2)}) copy-start(f32[48,64]{1,0:T(8,128)S(1)} %get-tuple-element.186) | copy-start | bytes 36868
  119.6 10.5 %copy-start.37 = (f32[48,64]{1,0:T(8,128)}, f32[48,64]{1,0:T(8,128)S(1)}, u32[]{:S(2)}) copy-start(f32[48,64]{1,0:T(8,128)S(1)} %get-tuple-element.188) | copy-start | bytes 36868
  119.6 10.5 %copy-start.38 = (f32[48,64]{1,0:T(8,128)}, f32[48,64]{1,0:T(8,128)S(1)}, u32[]{:S(2)}) copy-start(f32[48,64]{1,0:T(8,128)S(1)} %get-tuple-element.189) | copy-start | bytes 36868
  119.6 10.5 %copy-start.39 = (f32[48,64]{1,0:T(8,128)}, f32[48,64]{1,0:T(8,128)S(1)}, u32[]{:S(2)}) copy-start(f32[48,64]{1,0:T(8,128)S(1)} %get-tuple-element.190) | copy-start | bytes 36868
  119.6 16.3 %copy-start.15 = (f32[48,64]{1,0:T(8,128)}, f32[48,64]{1,0:T(8,128)S(1)}, u32[]{:S(2)}) copy-start(f32[48,64]{1,0:T(8,128)S(1)} %get-tuple-element.187) | copy-start | bytes 36868
  119.7 19.8 %copy-start.33 = (f32[48,64]{1,0:T(8,128)}, f32[48,64]{1,0:T(8,128)S(1)}, u32[]{:S(2)}) copy-start(f32[48,64]{1,0:T(8,128)S(1)} %get-tuple-element.183) | copy-start | bytes 36868
  119.7 19.8 %copy-start.34 = (f32[48,64]{1,0:T(8,128)}, f32[48,64]{1,0:T(8,128)S(1)}, u32[]{:S(2)}) copy-start(f32[48,64]{1,0:T(8,128)S(1)} %get-tuple-element.184) | copy-start | bytes 36868
  119.7 19.8 %copy-start.35 = (f32[48,64]{1,0:T(8,128)}, f32[48,64]{1,0:T(8,128)S(1)}, u32[]{:S(2)}) copy-start(f32[48,64]{1,0:T(8,128)S(1)} %get-tuple-element.185) | copy-start | bytes 36868
  130.0 9.5 %copy-start.19 = (f32[48,1,128]{2,1,0:T(1,128)}, f32[48,1,128]{2,1,0:T(1,128)S(1)}, u32[]{:S(2)}) copy-start(f32[48,1,128]{2,1,0:T(1,128)S(1)} %get-tuple-element.170) | copy-start | bytes 73732
  130.0 9.5 %copy-start.20 = (f32[48,1,128]{2,1,0:T(1,128)}, f32[48,1,128]{2,1,0:T(1,128)S(1)}, u32[]{:S(2)}) copy-start(f32[48,1,128]{2,1,0:T(1,128)S(1)} %get-tuple-element.171) | copy-start | bytes 73732
  164.5 197.4 %reduce-scatter.4.cloned.1.call-start = ((), (), s32[]{:S(2)}) async-start(), calls=%async_computation.4 | async-start | bytes 4423680
  264.6 9.6 %copy-start.57 = (f32[48]{0:T(128)}, f32[48]{0:T(128)S(1)}, u32[]{:S(2)}) copy-start(f32[48]{0:T(128)S(1)} %get-tuple-element.52) | copy-start | bytes 580
  264.6 14.8 %copy-start.69 = (f32[48]{0:T(128)}, f32[48]{0:T(128)S(1)}, u32[]{:S(2)}) copy-start(f32[48]{0:T(128)S(1)} %get-tuple-element.48) | copy-start | bytes 580
  264.6 14.8 %copy-start.70 = (f32[48]{0:T(128)}, f32[48]{0:T(128)S(1)}, u32[]{:S(2)}) copy-start(f32[48]{0:T(128)S(1)} %get-tuple-element.49) | copy-start | bytes 580
  264.7 14.8 %copy-start.71 = (f32[48]{0:T(128)}, f32[48]{0:T(128)S(1)}, u32[]{:S(2)}) copy-start(f32[48]{0:T(128)S(1)} %get-tuple-element.50) | copy-start | bytes 580
  267.5 11.9 %copy-start.26 = (f32[48,1,128]{2,1,0:T(1,128)}, f32[48,1,128]{2,1,0:T(1,128)S(1)}, u32[]{:S(2)}) copy-start(f32[48,1,128]{2,1,0:T(1,128)S(1)} %get-tuple-element.145) | copy-start | bytes 73732
  267.5 11.9 %copy-start.27 = (f32[48,1,128]{2,1,0:T(1,128)}, f32[48,1,128]{2,1,0:T(1,128)S(1)}, u32[]{:S(2)}) copy-start(f32[48,1,128]{2,1,0:T(1,128)S(1)} %get-tuple-element.146) | copy-start | bytes 73732
  267.6 11.9 %copy-start.28 = (f32[48,1,128]{2,1,0:T(1,128)}, f32[48,1,128]{2,1,0:T(1,128)S(1)}, u32[]{:S(2)}) copy-start(f32[48,1,128]{2,1,0:T(1,128)S(1)} %get-tuple-element.147) | copy-start | bytes 73732
  268.6 10.9 %copy-start.40 = (f32[48,64]{1,0:T(8,128)}, f32[48,64]{1,0:T(8,128)S(1)}, u32[]{:S(2)}) copy-start(f32[48,64]{1,0:T(8,128)S(1)} %bitcast_multiply_fusion.2) | copy-start | bytes 36868
  268.7 10.7 %copy-start.41 = (f32[48,64]{1,0:T(8,128)}, f32[48,64]{1,0:T(8,128)S(1)}, u32[]{:S(2)}) copy-start(f32[48,64]{1,0:T(8,128)S(1)} %get-tuple-element.158) | copy-start | bytes 36868
  268.8 10.7 %copy-start.42 = (f32[48,64]{1,0:T(8,128)}, f32[48,64]{1,0:T(8,128)S(1)}, u32[]{:S(2)}) copy-start(f32[48,64]{1,0:T(8,128)S(1)} %get-tuple-element.159) | copy-start | bytes 36868
  275.9 12.8 %copy-start.8 = (bf16[48,8,1,1,64]{4,3,1,0,2:T(2,128)(2,1)S(1)}, bf16[48,8,1,1,64]{4,3,1,0,2:T(2,128)(2,1)}, u32[]{:S(2)}) copy-start(bf16[48,8,1,1,64]{4,3,1,0,2:T(2,128)(2,1)} %get-tuple-element.140) | copy-start | bytes 147460
  275.9 30.1 %copy-start.74 = (f32[64]{0:T(128)S(1)}, f32[64]{0:T(128)}, u32[]{:S(2)}) copy-start(f32[64]{0:T(128)} %get-tuple-element.209) | copy-start | bytes 772
  (42 other events, 176.9 us)
Sparse Core Ops, SparseCore 0:
  60.1 32.7 all-gather.6
  94.5 32.6 all-gather.4
  164.6 89.6 all-reduce.1
  316.4 45.5 reduce-scatter.3
where the time goes:
time: 374 us; the launch traced here: 372 us
  waiting for transfers between devices  110 us (29%)
  local copies, waits for them, and re-layouts  81.8 us (22%)
  other arithmetic  75.7 us (20%)
  blocking collectives  74.6 us (20%)
  between operations  15.4 us (4%)
  matrix products  14.1 us (4%)
    psum x1, waiting for transfers between devices, local(): total = lax.psum(term, 'heads')  85.9 us
    unnamed x181, local copies, waits for them, and re-layouts  55.4 us
    psum x2, blocking collectives, token_scale(): return rms_scale(lax.psum(local_sq, 'heads'), inner)  30.6 us
    select_n x2, other arithmetic, recur(): kept = jnp.where((accepted == t + 1)[:, None, None], state, kept)  17.3 us
    all_gather x1, blocking collectives, local(): lax.all_gather(conv_bc_state, 'heads', axis=3, tiled=True)  16.7 us
    unnamed x5, waiting for transfers between devices  16.4 us
    all_gather x1, blocking collectives, local(): lax.all_gather(conv_bc_w, 'heads', axis=2, tiled=True)  15.1 us
    unnamed x14, other arithmetic  12.3 us
  transfers between devices with their start and end apart: 4, of which 3 were waited for; matrix products, arithmetic and copies ran while one was open for 13% of the time, Pallas kernels for 0%

commit v1 on v0

--- a/solution.py
+++ b/solution.py
@@ -155,7 +155,9 @@
             term = (
                 jnp.dot(u_rows, out_w[layer], preferred_element_type=jnp.float32) * scale[:, None]
             )
-            total = lax.psum(term, "heads")
+            total = term
+            for hop in (1, 2, 4):
+                total = total + lax.ppermute(total, "heads", [(dev, dev ^ hop) for dev in range(8)])
             stream = (stream.astype(jnp.float32) + total).astype(jnp.bfloat16)
         else:
             mine = lax.psum_scatter(

time: 374 us -> 551 us (1.47)
  waiting for transfers between devices: 110 us -> 286 us
    ppermute x0 -> x3, waiting for transfers between devices: none -> 262 us  [local(): lax.ppermute(total, 'heads', [(dev, dev ^ hop) for dev in range(8)])]
    psum x1 -> x0, waiting for transfers between devices: 85.9 us -> none  [local(): total = lax.psum(term, 'heads')]
    unnamed x5 -> x4, waiting for transfers between devices: 16.4 us -> 16.4 us
  transfers between devices with their start and end apart: 4 -> 6, of which waited for: 3 -> 5; matrix products, arithmetic and copies ran while one was open for 13% -> 9% of each run, Pallas kernels for 0% -> 0%
where the time goes in v1:
time: 551 us; the launch traced here: 548 us
  waiting for transfers between devices  286 us (52%)
  local copies, waits for them, and re-layouts  81.8 us (15%)
  other arithmetic  80.3 us (15%)
  blocking collectives  72.7 us (13%)
  between operations  15.4 us (3%)
  matrix products  12.2 us (2%)
    ppermute x3, waiting for transfers between devices, local(): lax.ppermute(total, 'heads', [(dev, dev ^ hop) for dev in range(8)])  262 us
    unnamed x181, local copies, waits for them, and re-layouts  55.4 us
    psum x2, blocking collectives, token_scale(): return rms_scale(lax.psum(local_sq, 'heads'), inner)  28.8 us
    select_n x2, other arithmetic, recur(): kept = jnp.where((accepted == t + 1)[:, None, None], state, kept)  17.3 us
    all_gather x1, blocking collectives, local(): lax.all_gather(conv_bc_state, 'heads', axis=3, tiled=True)  16.7 us
    unnamed x4, waiting for transfers between devices  16.4 us
    all_gather x1, blocking collectives, local(): lax.all_gather(conv_bc_w, 'heads', axis=2, tiled=True)  15.1 us
    unnamed x14, other arithmetic  12.3 us
  transfers between devices with their start and end apart: 6, of which 5 were waited for; matrix products, arithmetic and copies ran while one was open for 9% of the time, Pallas kernels for 0%

profile of v1, /device:TPU:0, one launch (start us, length us, event | category | flops | bytes accessed | tf_op | source)
XLA Modules:
  0.0 548.3 jit_solution(18234454257303479747)
XLA Ops:
  7.2 43.7 %copy.113 = bf16[50280,320]{1,0:T(8,128)(2,1)} copy(bf16[50280,320]{0,1:T(8,128)(2,1)} %param.21) | data formatting | bytes 64358400 | tf_op args[2]
  51.2 7.8 %gather_fusion = bf16[384,320]{1,0:T(8,128)(2,1)S(1)} fusion(bf16[50280,320]{1,0:T(8,128)(2,1)} %copy.113, s32[1024]{0:T(1024)S(1)} %pad_clamp_fusion), kind=kCustom, calls=%fused_computation | custom fusion | bytes 493056 | tf_op jit(solution)/shard_map/gather | solution.py:147
  60.8 16.7 %all_gather.16 = bf16[2,48,3,256]{1,3,2,0:T(8,128)(2,1)S(1)} all-gather(bf16[2,48,3,32]{1,3,2,0:T(8,128)(2,1)S(1)} %copy-done.48), channel_id=1, replica_groups=mesh['batch'=4,'heads'=8] {'heads'}, dimensions={3}, use_global_device_ids=true | all-gather | bytes 165888 | tf_op jit(solution)/shard_map/all_gather | solution.py:91
  77.9 15.1 %all_gather.18 = bf16[2,4,256]{1,0,2:T(2,128)(2,1)S(1)} all-gather(bf16[2,4,32]{1,0,2:T(2,128)(2,1)S(1)} %copy.118), channel_id=1, replica_groups=mesh['batch'=4,'heads'=8] {'heads'}, dimensions={2}, use_global_device_ids=true | all-gather | bytes 4608 | tf_op jit(solution)/shard_map/all_gather | solution.py:89
  93.0 12.0 %all-gather.1 = bf16[8,32,2]{1,2,0:T(2,128)(2,1)S(1)} all-gather(bf16[1,32,2]{1,2,0:T(2,128)(2,1)S(1)} %bitcast.580), channel_id=1, replica_groups=mesh['batch'=4,'heads'=8] {'heads'}, dimensions={0}, use_global_device_ids=true | all-gather | bytes 1152 | tf_op jit(solution)/shard_map/all_gather | solution.py:90
  107.1 2.9 slice_reduce_fusion.7
  111.3 2.7 copy.115
  119.7 7.5 %all-gather.5.cloned.1.call-done = bf16[2,2560,256]{1,2,0:T(8,128)(2,1)} async-done(((bf16[2,2560,32]{1,2,0:T(8,128)(2,1)}), bf16[2,2560,256]{1,2,0:T(8,128)(2,1)}) %all-gather.5.cloned.1.call-update) | async-done | bytes 2621456 | tf_op jit(solution)/shard_map/all_gather | solution.py:88
  127.2 2.0 fusion.15
  130.1 1.1 copy-done
  131.2 4.1 multiply_add_fusion.8
  136.0 1.6 multiply_reduce_fusion.12
  139.5 3.7 multiply_reduce_fusion.8
  145.9 15.2 %psum.14 = f32[384]{0:T(512)S(1)} all-reduce(f32[384]{0:T(512)S(1)} %reshape.2511), channel_id=1, replica_groups=mesh['batch'=4,'heads'=8] {'heads'}, use_global_device_ids=true, to_apply=%region_10.11 | all-reduce | flops 384 | bytes 3072 | tf_op jit(solution)/shard_map/psum | solution.py:53
  161.2 1.6 convolution_multiply_fusion.1
  162.9 6.8 %collective-permute-done = f32[384,2560]{1,0:T(8,128)S(1)} collective-permute-done((f32[384,2560]{1,0:T(8,128)S(1)}, f32[384,2560]{1,0:T(8,128)S(1)}, u32[]{:S(2)}, u32[]{:S(2)}) %collective-permute-start) | collective-permute-done | bytes 3932192 | tf_op jit(solution)/shard_map/ppermute | solution.py:160
  170.3 87.0 %collective-permute-done.1 = f32[384,2560]{1,0:T(8,128)S(1)} collective-permute-done((f32[384,2560]{1,0:T(8,128)S(1)}, f32[384,2560]{1,0:T(8,128)S(1)}, u32[]{:S(2)}, u32[]{:S(2)}) %collective-permute-start.1) | collective-permute-done | bytes 3932192 | tf_op jit(solution)/shard_map/ppermute | solution.py:160
  257.3 2.5 add.1165
  260.6 2.9 slice_reduce_fusion.3
  263.5 167.9 %collective-permute-done.2 = f32[384,2560]{1,0:T(8,128)} collective-permute-done((f32[384,2560]{1,0:T(8,128)}, f32[384,2560]{1,0:T(8,128)}, u32[]{:S(2)}, u32[]{:S(2)}) %collective-permute-start.2) | collective-permute-done | bytes 3932192 | tf_op jit(solution)/shard_map/ppermute | solution.py:160
  431.4 4.2 fusion.1
  443.0 2.1 fusion.14
  447.2 4.1 multiply_add_fusion.2
  451.3 1.2 constant_dynamic-update-slice_fusion.23
  452.5 1.6 multiply_reduce_fusion.4
  454.2 1.2 constant_dynamic-update-slice_fusion.22
  455.4 1.2 constant_dynamic-update-slice_fusion.21
  456.6 1.2 constant_dynamic-update-slice_fusion.20
  457.8 4.0 multiply_reduce_fusion
  461.8 1.2 constant_dynamic-update-slice_fusion.19
  463.0 1.2 constant_dynamic-update-slice_fusion.18
  464.1 1.2 constant_dynamic-update-slice_fusion.17
  465.3 1.9 constant_dynamic-update-slice_fusion.16
  468.9 13.6 %psum.15 = f32[384]{0:T(512)S(1)} all-reduce(f32[384]{0:T(512)S(1)} %reshape.2516), channel_id=1, replica_groups=mesh['batch'=4,'heads'=8] {'heads'}, use_global_device_ids=true, to_apply=%region_21.22 | all-reduce | flops 384 | bytes 3072 | tf_op jit(solution)/shard_map/psum | solution.py:53
  482.5 1.1 fusion.71
  483.6 3.5 fusion
  487.1 5.6 %copy.139 = f32[2560,384]{1,0:T(8,128)} copy(f32[2560,384]{0,1:T(8,128)} %fusion) | data formatting | bytes 7864320
  492.7 1.2 broadcast_compare_fusion.7
  494.0 1.7 fusion.105
  495.7 1.4 fusion.119
  498.5 9.0 %select_select_fusion.1 = f32[1,48,1,64,128]{4,3,2,1,0:T(8,128)} fusion(f32[2,48,1,64,128]{4,3,2,1,0:T(8,128)S(1)} %copy-done.1, f32[48,128]{1,0:T(8,128)} %bitcast.536, f32[48,64]{1,0:T(8,128)} %copy-done.34, f32[48,128]{1,0:T(8,128)} %bitcast.534, f32[48,64]{1,0:T(8,128)} %copy-done.35, f32[48,128]{1,0:T(8,128)} %bitcast.532, f32[48,64]{1,0:T(8,128)} %copy-done.33, ...), kind=kLoop, calls=%fused_computation.22 | loop fusion | flops 12582912 | bytes 3442560 | tf_op jit(solution)/shard_map/vmap(jit(_where))/select_n | solution.py:41
  508.9 1.4 pad_maximum_fusion.6
  511.2 1.4 pad_maximum_fusion.5
  512.6 8.2 %select_select_fusion = f32[1,48,1,64,128]{4,3,2,1,0:T(8,128)S(1)} fusion(f32[2,48,1,64,128]{4,3,2,1,0:T(8,128)S(1)} %copy-done.1, f32[48,128]{1,0:T(8,128)} %bitcast.550, f32[48,64]{1,0:T(8,128)} %copy-done.40, f32[48,128]{1,0:T(8,128)} %bitcast.548, f32[48,64]{1,0:T(8,128)} %copy-done.42, f32[48,128]{1,0:T(8,128)} %bitcast.546, f32[48,64]{1,0:T(8,128)} %copy-done.41, ...), kind=kLoop, calls=%fused_computation.21 | loop fusion | flops 12582912 | bytes 3442560 | tf_op jit(solution)/shard_map/vmap(jit(_where))/select_n | solution.py:41
  520.9 1.9 pad_maximum_fusion
  522.8 15.7 %reduce-scatter.4.cloned.1.call-done = f32[320,384]{1,0:T(8,128)} async-done(((f32[2560,384]{1,0:T(8,128)}), f32[320,384]{1,0:T(8,128)}) %reduce-scatter.4.cloned.1.call-update) | async-done | bytes 491536
  538.5 1.3 copy.140
  539.8 1.2 fusion.20
  (264 shorter events, 33.5 us)
Async XLA Ops:
  7.2 43.8 %copy-start.73 = (s32[48,8]{0,1:T(8,128)S(1)}, s32[48,8]{0,1:T(8,128)}, u32[]{:S(2)}) copy-start(s32[48,8]{0,1:T(8,128)} %param.19) | copy-start | bytes 4612
  7.2 104.1 %all-gather.7.cloned.1.call-start = ((), (), s32[]{:S(2)}) async-start(), calls=%async_computation.2 | async-start | bytes 2211840 | tf_op jit(solution)/shard_map/all_gather | solution.py:148
  51.2 9.7 %copy-start.48 = (bf16[2,48,3,32]{1,3,2,0:T(8,128)(2,1)S(1)}, bf16[2,48,3,32]{1,3,2,0:T(8,128)(2,1)}, u32[]{:S(2)}) copy-start(bf16[2,48,3,32]{1,3,2,0:T(8,128)(2,1)} %param.37) | copy-start | bytes 55300
  59.0 18.7 %copy-start.75 = (bf16[2,4,32]{2,1,0:T(4,128)(2,1)S(1)}, bf16[2,4,32]{2,1,0:T(4,128)(2,1)}, u32[]{:S(2)}) copy-start(bf16[2,4,32]{2,1,0:T(4,128)(2,1)} %param.31) | copy-start | bytes 1540
  59.0 34.0 %copy-start.82 = (bf16[2,32]{1,0:T(2,128)(2,1)S(1)}, bf16[2,32]{1,0:T(2,128)(2,1)}, u32[]{:S(2)}) copy-start(bf16[2,32]{1,0:T(2,128)(2,1)} %param.32) | copy-start | bytes 388
  59.0 46.1 %copy-start.77 = (f32[2,1]{0,1:T(1,128)S(1)}, f32[2,1]{0,1:T(1,128)}, u32[]{:S(2)}) copy-start(f32[2,1]{0,1:T(1,128)} %param.26) | copy-start | bytes 28
  59.0 46.7 %copy-start.78 = (f32[2,1]{0,1:T(1,128)S(1)}, f32[2,1]{0,1:T(1,128)}, u32[]{:S(2)}) copy-start(f32[2,1]{0,1:T(1,128)} %param.27) | copy-start | bytes 28
  59.1 47.3 %copy-start.79 = (f32[2,1]{0,1:T(1,128)S(1)}, f32[2,1]{0,1:T(1,128)}, u32[]{:S(2)}) copy-start(f32[2,1]{0,1:T(1,128)} %param.28) | copy-start | bytes 28
  59.1 47.8 %copy-start.55 = (f32[2,2560]{1,0:T(2,128)S(1)}, f32[2,2560]{1,0:T(2,128)}, u32[]{:S(2)}) copy-start(f32[2,2560]{1,0:T(2,128)} %param.22) | copy-start | bytes 61444
  60.0 50.1 %copy-start.80 = (bf16[2,64]{1,0:T(2,128)(2,1)S(1)}, bf16[2,64]{1,0:T(2,128)(2,1)}, u32[]{:S(2)}) copy-start(bf16[2,64]{1,0:T(2,128)(2,1)} %param.30) | copy-start | bytes 772
  60.0 50.1 %copy-start.81 = (f32[2,64]{1,0:T(2,128)S(1)}, f32[2,64]{1,0:T(2,128)}, u32[]{:S(2)}) copy-start(f32[2,64]{1,0:T(2,128)} %param.33) | copy-start | bytes 1540
  60.0 51.2 %copy-start.76 = (bf16[2,4,64]{2,1,0:T(4,128)(2,1)S(1)}, bf16[2,4,64]{2,1,0:T(4,128)(2,1)}, u32[]{:S(2)}) copy-start(bf16[2,4,64]{2,1,0:T(4,128)(2,1)} %param.29) | copy-start | bytes 3076
  60.0 51.2 %copy-start.47 = (bf16[2,48,3,64]{3,1,2,0:T(8,128)(2,1)S(1)}, bf16[2,48,3,64]{3,1,2,0:T(8,128)(2,1)}, u32[]{:S(2)}) copy-start(bf16[2,48,3,64]{3,1,2,0:T(8,128)(2,1)} %param.36) | copy-start | bytes 110596
  60.0 67.2 %all-gather.5.cloned.1.call-start = ((), (), s32[]{:S(2)}) async-start(), calls=%async_computation.1 | async-start | bytes 2949120 | tf_op jit(solution)/shard_map/all_gather | solution.py:88
  60.8 477.7 %reduce-scatter.4.cloned.1.call-start = ((), (), s32[]{:S(2)}) async-start(), calls=%async_computation.3 | async-start | bytes 4423680
  77.8 51.5 %copy-start.10 = (bf16[48,3,256]{2,1,0:T(4,128)(2,1)}, bf16[48,3,256]{2,1,0:T(4,128)(2,1)S(1)}, u32[]{:S(2)}) copy-start(bf16[48,3,256]{2,1,0:T(4,128)(2,1)S(1)} %copy.117) | copy-start | bytes 221188
  111.3 327.5 %copy-start.17 = (bf16[48,3,64]{2,0,1:T(8,128)(2,1)}, bf16[48,3,64]{2,0,1:T(8,128)(2,1)S(1)}, u32[]{:S(2)}) copy-start(bf16[48,3,64]{2,0,1:T(8,128)(2,1)S(1)} %get-tuple-element.193) | copy-start | bytes 55300
  119.2 10.8 %copy-start.58 = (f32[48]{0:T(128)}, f32[48]{0:T(128)S(1)}, u32[]{:S(2)}) copy-start(f32[48]{0:T(128)S(1)} %get-tuple-element.233) | copy-start | bytes 580
  119.2 10.8 %copy-start.59 = (f32[48]{0:T(128)}, f32[48]{0:T(128)S(1)}, u32[]{:S(2)}) copy-start(f32[48]{0:T(128)S(1)} %get-tuple-element.234) | copy-start | bytes 580
  119.2 10.8 %copy-start.60 = (f32[48]{0:T(128)}, f32[48]{0:T(128)S(1)}, u32[]{:S(2)}) copy-start(f32[48]{0:T(128)S(1)} %get-tuple-element.235) | copy-start | bytes 580
  119.3 10.8 %copy-start.61 = (f32[48]{0:T(128)}, f32[48]{0:T(128)S(1)}, u32[]{:S(2)}) copy-start(f32[48]{0:T(128)S(1)} %get-tuple-element.237) | copy-start | bytes 580
  119.3 16.7 %copy-start.56 = (f32[48]{0:T(128)}, f32[48]{0:T(128)S(1)}, u32[]{:S(2)}) copy-start(f32[48]{0:T(128)S(1)} %get-tuple-element.236) | copy-start | bytes 580
  119.3 20.1 %copy-start.66 = (f32[48]{0:T(128)}, f32[48]{0:T(128)S(1)}, u32[]{:S(2)}) copy-start(f32[48]{0:T(128)S(1)} %get-tuple-element.238) | copy-start | bytes 580
  119.3 20.1 %copy-start.67 = (f32[48]{0:T(128)}, f32[48]{0:T(128)S(1)}, u32[]{:S(2)}) copy-start(f32[48]{0:T(128)S(1)} %get-tuple-element.239) | copy-start | bytes 580
  119.3 20.1 %copy-start.68 = (f32[48]{0:T(128)}, f32[48]{0:T(128)S(1)}, u32[]{:S(2)}) copy-start(f32[48]{0:T(128)S(1)} %get-tuple-element.240) | copy-start | bytes 580
  119.6 10.5 %copy-start.36 = (f32[48,64]{1,0:T(8,128)}, f32[48,64]{1,0:T(8,128)S(1)}, u32[]{:S(2)}) copy-start(f32[48,64]{1,0:T(8,128)S(1)} %get-tuple-element.186) | copy-start | bytes 36868
  119.6 10.5 %copy-start.37 = (f32[48,64]{1,0:T(8,128)}, f32[48,64]{1,0:T(8,128)S(1)}, u32[]{:S(2)}) copy-start(f32[48,64]{1,0:T(8,128)S(1)} %get-tuple-element.188) | copy-start | bytes 36868
  119.6 10.5 %copy-start.38 = (f32[48,64]{1,0:T(8,128)}, f32[48,64]{1,0:T(8,128)S(1)}, u32[]{:S(2)}) copy-start(f32[48,64]{1,0:T(8,128)S(1)} %get-tuple-element.189) | copy-start | bytes 36868
  119.6 10.5 %copy-start.39 = (f32[48,64]{1,0:T(8,128)}, f32[48,64]{1,0:T(8,128)S(1)}, u32[]{:S(2)}) copy-start(f32[48,64]{1,0:T(8,128)S(1)} %get-tuple-element.190) | copy-start | bytes 36868
  119.6 16.3 %copy-start.15 = (f32[48,64]{1,0:T(8,128)}, f32[48,64]{1,0:T(8,128)S(1)}, u32[]{:S(2)}) copy-start(f32[48,64]{1,0:T(8,128)S(1)} %get-tuple-element.187) | copy-start | bytes 36868
  119.7 19.8 %copy-start.33 = (f32[48,64]{1,0:T(8,128)}, f32[48,64]{1,0:T(8,128)S(1)}, u32[]{:S(2)}) copy-start(f32[48,64]{1,0:T(8,128)S(1)} %get-tuple-element.183) | copy-start | bytes 36868
  119.7 19.8 %copy-start.34 = (f32[48,64]{1,0:T(8,128)}, f32[48,64]{1,0:T(8,128)S(1)}, u32[]{:S(2)}) copy-start(f32[48,64]{1,0:T(8,128)S(1)} %get-tuple-element.184) | copy-start | bytes 36868
  119.7 19.8 %copy-start.35 = (f32[48,64]{1,0:T(8,128)}, f32[48,64]{1,0:T(8,128)S(1)}, u32[]{:S(2)}) copy-start(f32[48,64]{1,0:T(8,128)S(1)} %get-tuple-element.185) | copy-start | bytes 36868
  162.8 6.8 %collective-permute-start = (f32[384,2560]{1,0:T(8,128)S(1)}, f32[384,2560]{1,0:T(8,128)S(1)}, u32[]{:S(2)}, u32[]{:S(2)}) collective-permute-start(f32[384,2560]{1,0:T(8,128)S(1)} %convolution_multiply_fusion.1), channel_id=1, source_target_pairs={{0,1},{1,0},{2,3},{3,2},{4,5},{5,4},{6,7},{7,6},{8,9},{9,8},{10,11... | collective-permute-start | bytes 11796488 | tf_op jit(solution)/shard_map/ppermute | solution.py:160
  170.3 87.1 %collective-permute-start.1 = (f32[384,2560]{1,0:T(8,128)S(1)}, f32[384,2560]{1,0:T(8,128)S(1)}, u32[]{:S(2)}, u32[]{:S(2)}) collective-permute-start(f32[384,2560]{1,0:T(8,128)S(1)} %add.1164), channel_id=1, source_target_pairs={{0,2},{1,3},{2,0},{3,1},{4,6},{5,7},{6,4},{7,5},{8,10},{9,11},{10,... | collective-permute-start | bytes 11796488 | tf_op jit(solution)/shard_map/ppermute | solution.py:160
  259.8 171.6 %collective-permute-start.2 = (f32[384,2560]{1,0:T(8,128)}, f32[384,2560]{1,0:T(8,128)}, u32[]{:S(2)}, u32[]{:S(2)}) collective-permute-start(f32[384,2560]{1,0:T(8,128)} %add.1165), channel_id=1, source_target_pairs={{0,4},{1,5},{2,6},{3,7},{4,0},{5,1},{6,2},{7,3},{8,12},{9,13},{10,... | collective-permute-start | bytes 11796488 | tf_op jit(solution)/shard_map/ppermute | solution.py:160
  263.5 172.1 %copy-start.84 = (bf16[2,2560,1,128]{3,1,2,0:T(8,128)(2,1)S(1)}, bf16[2,2560,1,128]{3,1,2,0:T(8,128)(2,1)}, u32[]{:S(2)}) copy-start(bf16[2,2560,1,128]{3,1,2,0:T(8,128)(2,1)} %param.23) | copy-start | bytes 3932164
  442.9 14.8 %copy-start.69 = (f32[48]{0:T(128)}, f32[48]{0:T(128)S(1)}, u32[]{:S(2)}) copy-start(f32[48]{0:T(128)S(1)} %get-tuple-element.48) | copy-start | bytes 580
  442.9 14.8 %copy-start.70 = (f32[48]{0:T(128)}, f32[48]{0:T(128)S(1)}, u32[]{:S(2)}) copy-start(f32[48]{0:T(128)S(1)} %get-tuple-element.49) | copy-start | bytes 580
  443.0 14.8 %copy-start.71 = (f32[48]{0:T(128)}, f32[48]{0:T(128)S(1)}, u32[]{:S(2)}) copy-start(f32[48]{0:T(128)S(1)} %get-tuple-element.50) | copy-start | bytes 580
  445.8 11.9 %copy-start.26 = (f32[48,1,128]{2,1,0:T(1,128)}, f32[48,1,128]{2,1,0:T(1,128)S(1)}, u32[]{:S(2)}) copy-start(f32[48,1,128]{2,1,0:T(1,128)S(1)} %get-tuple-element.145) | copy-start | bytes 73732
  445.9 11.9 %copy-start.27 = (f32[48,1,128]{2,1,0:T(1,128)}, f32[48,1,128]{2,1,0:T(1,128)S(1)}, u32[]{:S(2)}) copy-start(f32[48,1,128]{2,1,0:T(1,128)S(1)} %get-tuple-element.146) | copy-start | bytes 73732
  445.9 11.9 %copy-start.28 = (f32[48,1,128]{2,1,0:T(1,128)}, f32[48,1,128]{2,1,0:T(1,128)S(1)}, u32[]{:S(2)}) copy-start(f32[48,1,128]{2,1,0:T(1,128)S(1)} %get-tuple-element.147) | copy-start | bytes 73732
  446.9 10.9 %copy-start.40 = (f32[48,64]{1,0:T(8,128)}, f32[48,64]{1,0:T(8,128)S(1)}, u32[]{:S(2)}) copy-start(f32[48,64]{1,0:T(8,128)S(1)} %bitcast_multiply_fusion.2) | copy-start | bytes 36868
  447.1 10.7 %copy-start.41 = (f32[48,64]{1,0:T(8,128)}, f32[48,64]{1,0:T(8,128)S(1)}, u32[]{:S(2)}) copy-start(f32[48,64]{1,0:T(8,128)S(1)} %get-tuple-element.158) | copy-start | bytes 36868
  447.1 10.7 %copy-start.42 = (f32[48,64]{1,0:T(8,128)}, f32[48,64]{1,0:T(8,128)S(1)}, u32[]{:S(2)}) copy-start(f32[48,64]{1,0:T(8,128)S(1)} %get-tuple-element.159) | copy-start | bytes 36868
  454.2 13.1 %copy-start.8 = (bf16[48,8,1,1,64]{4,3,1,0,2:T(2,128)(2,1)S(1)}, bf16[48,8,1,1,64]{4,3,1,0,2:T(2,128)(2,1)}, u32[]{:S(2)}) copy-start(bf16[48,8,1,1,64]{4,3,1,0,2:T(2,128)(2,1)} %get-tuple-element.140) | copy-start | bytes 147460
  454.2 28.3 %copy-start.74 = (f32[64]{0:T(128)S(1)}, f32[64]{0:T(128)}, u32[]{:S(2)}) copy-start(f32[64]{0:T(128)} %get-tuple-element.209) | copy-start | bytes 772
  (44 other events, 202.5 us)
Sparse Core Ops, SparseCore 0:
  60.1 32.7 all-gather.6
  94.5 32.6 all-gather.4
  492.9 45.5 reduce-scatter.3
